TPU v7x, 1024 devices: a whole 4x8x16 slice. The times are simulated.
1024 devices in a mesh: grp: 4 (over x), row: 16 (over y, core), col: 16 (over z).
Axes of the slice: x: 4, y: 8, z: 16, core: 2. Of those that a mesh axis runs over, the one named last changes fastest.
Arguments:
- gradients: bfloat16 [4, 3072, 24576], P('grp', 'row', 'col'), may hold values from -6 to 6
- momentum: float32 [4, 3072, 24576], P('grp', 'row', 'col'), may hold values from -94 to 94, as said below
- right_basis: bfloat16 [24576, 512], P('col'), may hold values from -6 to 6
Outputs:
- new_momentum: float32 [4, 3072, 24576], P('grp', 'row', 'col')
- new_basis: bfloat16 [24576, 512], P('col')
- update: bfloat16 [3072, 24576], P('row', 'col')
Inputs may be any that keep to these rules, and one draw needn't show every extreme that they name: Each group's momentum buffer holds real values bounded in magnitude by 94.
All inputs are finite; a program needn't handle non-finite values.
Results may differ from a plain program's by a relative error of at most 0.013.
Values may be sent and summed in bfloat16 or wider, within the bound.
A program may use at most 32 MiB of HBM per device.

v0:
```python
import math

import jax
import jax.numpy as jnp
from jax import lax
from jax.sharding import Mesh
from jax.sharding import PartitionSpec as P

D = 3072
FF = 24576
ROW = ("row_0", "row_1")
GRP_ROW = ("grp", "row_0", "row_1")
GRP_ROW_COL = ("grp", "row_0", "row_1", "col")


momentum_decay = 0.9
ridge_scale = 0.0001
epsilon = 1e-06


def rows_for(lines, devices):
    spare = -len(lines) % devices
    return jnp.pad(lines, [(0, spare)] + [(0, 0)] * (lines.ndim - 1))


def reduced_to_own(tiles, axes, order):
    dims = [lax.axis_size(a) for a in axes]
    tiles = tiles.reshape(*dims, *tiles.shape[1:])
    tiles = tiles.transpose(*order, *range(len(axes), tiles.ndim))
    tiles = tiles.reshape(-1, *tiles.shape[len(axes) :])
    for k in order:
        tiles = lax.psum_scatter(tiles, axes[k], scatter_dimension=0, tiled=True)
    return tiles[0]


def gather_in_order(shard, axes, order):
    tiles = shard
    for k in order:
        tiles = lax.all_gather(tiles, axes[k])
    done = order[::-1]
    back = [done.index(k) for k in range(len(axes))]
    tiles = tiles.transpose(*back, *range(len(axes), tiles.ndim))
    return tiles.reshape(-1, *shard.shape)


def sum_by_parts(shard, axes, order):
    devices, lines = (lax.axis_size(axes), shard.reshape(-1, *shard.shape[1:][-1:]))
    tiles = rows_for(lines, devices).reshape(devices, -1, *lines.shape[1:])
    own = reduced_to_own(tiles, axes, order)
    whole = gather_in_order(own, axes, order[::-1]).reshape(-1, *lines.shape[1:])
    return whole[: len(lines)].reshape(shard.shape)


def in_blocks(shard, dim, devices):
    before, after = (shard.shape[:dim], shard.shape[dim + 1 :])
    return jnp.moveaxis(shard.reshape(*before, devices, -1, *after), dim, 0)


def sent_and_summed(shard, axis, dim):
    tiles = in_blocks(shard, dim, lax.axis_size(axis))
    arrived = lax.all_to_all(tiles, axis, split_axis=0, concat_axis=0, tiled=True)
    return arrived.sum(axis=0)


def by_axis(shard, axes):
    for axis in axes:
        shard = lax.psum(shard, axis)
    return shard


def per_device(gradients, momentum, right_basis):
    merged = momentum[0] + gradients[0].astype(jnp.float32)
    merged_low = merged.astype(jnp.bfloat16)
    rank = right_basis.shape[1]
    local_rows = merged.shape[0]
    groups = lax.axis_size("grp")
    left_factor = jnp.dot(merged_low, right_basis, preferred_element_type=jnp.float32)
    left_factor = lax.psum(left_factor, ("grp", "col"))
    gram_matrix = jnp.dot(
        left_factor.T,
        left_factor,
        precision=lax.Precision.HIGHEST,
        preferred_element_type=jnp.float32,
    )
    gram_matrix = sum_by_parts(gram_matrix, ROW, (0, 1))
    shifted = gram_matrix + ridge_scale * (jnp.trace(gram_matrix) / rank) * jnp.eye(
        rank, dtype=jnp.float32
    )
    cholesky_factor = jnp.linalg.cholesky(shifted)
    orthonormal = jax.scipy.linalg.solve_triangular(cholesky_factor, left_factor.T, lower=True).T
    orthonormal_low = orthonormal.astype(jnp.bfloat16)
    right_piece = sent_and_summed(
        jnp.einsum("ij,ik->jk", merged_low, orthonormal_low, preferred_element_type=jnp.float32)
        / groups,
        GRP_ROW,
        0,
    )
    squares_sum = by_axis(jnp.sum(right_piece * right_piece, axis=0), GRP_ROW_COL)
    column_rms = jnp.sqrt(squares_sum / FF + epsilon)
    basis_piece = (right_piece / column_rms).astype(jnp.bfloat16)
    new_basis = lax.all_gather(basis_piece, GRP_ROW, axis=0, tiled=True)
    scaled_low = (orthonormal * column_rms).astype(jnp.bfloat16)
    stacked_left = jnp.concatenate([orthonormal_low, scaled_low], axis=0)
    products = lax.dot_general(
        stacked_left, new_basis, (((1,), (1,)), ((), ())), preferred_element_type=jnp.float32
    )
    update = (math.sqrt(D / rank) * products[:local_rows]).astype(jnp.bfloat16)
    new_momentum = merged - (1 - momentum_decay) * products[local_rows:]
    return (new_momentum[None], new_basis, update)


def solution(mesh):
    torus = Mesh(
        mesh.devices.reshape(mesh.shape["grp"], 8, 2, mesh.shape["col"]),
        ("grp", "row_0", "row_1", "col"),
    )
    return jax.shard_map(
        per_device,
        mesh=torus,
        in_specs=(P("grp", ROW, "col"), P("grp", ROW, "col"), P("col", None)),
        out_specs=(P("grp", ROW, "col"), P("col", None), P(ROW, "col")),
        check_vma=False,
    )
```

profile of v0, /device:TPU:1, one launch (start us, length us, event | category | flops | bytes accessed | tf_op | source)
XLA Modules:
  0.0 825.8 jit_solution(4313515153542348386)
XLA Ops:
  8.6 2.6 fusion.42
  11.3 279.4 %all-reduce.3.cloned.1.call-done = f32[192,512]{1,0:T(8,128)} async-done(((f32[192,512]{1,0:T(8,128)}), f32[192,512]{1,0:T(8,128)}) %all-reduce.3.cloned.1.call-update) | async-done | bytes 393232 | tf_op jit(solution)/shard_map/psum | solution.py:78
  290.7 3.2 fusion.44
  293.9 47.2 %reduce-scatter.3.cloned.1.call-done = f32[2,32,512]{2,1,0:T(8,128)} async-done(((f32[16,32,512]{2,1,0:T(8,128)}), f32[2,32,512]{2,1,0:T(8,128)}) %reduce-scatter.3.cloned.1.call-update) | async-done | bytes 131088 | tf_op jit(solution)/shard_map/reduce_scatter | solution.py:32
  341.2 31.4 %reduce-scatter.5.cloned.1.call-done = f32[1,32,512]{2,1,0:T(8,128)} async-done(((f32[2,32,512]{2,1,0:T(8,128)}), f32[1,32,512]{2,1,0:T(8,128)}) %reduce-scatter.5.cloned.1.call-update) | async-done | bytes 65552 | tf_op jit(solution)/shard_map/reduce_scatter | solution.py:32
  372.6 3.3 all_gather.12
  376.1 40.0 %all-gather.6.cloned.1.call-done = f32[16,32,512]{2,1,0:T(8,128)} async-done(((f32[2,32,512]{2,1,0:T(8,128)}), f32[16,32,512]{2,1,0:T(8,128)}) %all-gather.6.cloned.1.call-update) | async-done | bytes 1048592 | tf_op jit(solution)/shard_map/all_gather | solution.py:39
  421.6 2.5 copy.27
  426.5 11.7 %cholesky.103 = f32[128,128]{1,0:T(8,128)S(1)} custom-call(f32[128,128]{1,0:T(8,128)S(1)} %cholesky.263), custom_call_target="Cholesky" | custom-call | tf_op jit(solution)/shard_map/jit(cholesky)/cholesky | solution.py:89
  438.4 9.8 %custom-call.31 = f32[1,128,128]{1,2,0:T(8,128)S(1)} custom-call(f32[1,128,128]{2,1,0:T(8,128)S(1)} %get-tuple-element.40), custom_call_target="InvertDiagBlocksLowerTriangular" | custom-call | tf_op jit(solution)/shard_map/jit(cholesky)/cholesky | solution.py:89
  450.9 11.7 %cholesky.215 = f32[128,128]{1,0:T(8,128)S(1)} custom-call(f32[128,128]{1,0:T(8,128)S(1)} %cholesky.267), custom_call_target="Cholesky" | custom-call | tf_op jit(solution)/shard_map/jit(cholesky)/cholesky | solution.py:89
  462.7 9.9 %custom-call.32 = f32[1,128,128]{1,2,0:T(8,128)S(1)} custom-call(f32[1,128,128]{2,1,0:T(8,128)S(1)} %get-tuple-element.38), custom_call_target="InvertDiagBlocksLowerTriangular" | custom-call | tf_op jit(solution)/shard_map/jit(cholesky)/cholesky | solution.py:89
  474.6 11.7 %cholesky.236 = f32[128,128]{1,0:T(8,128)S(1)} custom-call(f32[128,128]{1,0:T(8,128)S(1)} %cholesky.272), custom_call_target="Cholesky" | custom-call | tf_op jit(solution)/shard_map/jit(cholesky)/cholesky | solution.py:89
  486.5 9.8 %custom-call.33 = f32[1,128,128]{1,2,0:T(8,128)S(1)} custom-call(f32[1,128,128]{2,1,0:T(8,128)S(1)} %get-tuple-element.36), custom_call_target="InvertDiagBlocksLowerTriangular" | custom-call | tf_op jit(solution)/shard_map/jit(cholesky)/cholesky | solution.py:89
  497.9 11.9 %cholesky.253 = f32[128,128]{1,0:T(8,128)S(1)} custom-call(f32[128,128]{1,0:T(8,128)S(1)} %convolution_subtract_fusion.5), custom_call_target="Cholesky" | custom-call | tf_op jit(solution)/shard_map/jit(cholesky)/cholesky | solution.py:89
  515.6 12.5 %while.1 = (s32[]{:T(128)}, f32[512,512]{0,1:T(8,128)}, s32[4,2]{0,1:T(2,128)S(1)}, f32[4,128,128]{2,1,0:T(8,128)S(1)}, s32[]{:T(128)}) while((s32[]{:T(128)}, f32[512,512]{0,1:T(8,128)}, s32[4,2]{0,1:T(2,128)S(1)}, f32[4,128,128]{2,1,0:T(8,128)S(1)}, s32[]{:T(128)}) %tuple.31), condition=%wide.while_cond, body=%wide.while_body.sunk | while | flops 2 | bytes 393329 | solution.py:90
  528.1 39.3 %custom-call.34 = f32[4,128,128]{1,2,0:T(8,128)S(1)} custom-call(f32[4,128,128]{2,1,0:T(8,128)S(1)} %get-tuple-element.10), custom_call_target="InvertDiagBlocksLowerTriangular" | custom-call | tf_op jit(solution)/shard_map/jit(_solve_triangular)/triangular_solve | solution.py:90
  577.3 86.3 %all_to_all.5 = f32[64,24,512]{2,1,0:T(8,128)} all-to-all(f32[64,24,512]{2,1,0:T(8,128)S(1)} %bitcast.66), channel_id=1, replica_groups=mesh['grp'=4,'row_0'=8,'row_1'=2,'col'=16] {'grp','row_0','row_1'}, dimensions={0} | all-to-all | bytes 6291456 | tf_op jit(solution)/shard_map/all_to_all | solution.py:61
  663.6 2.7 reduce_sum.29
  667.1 8.7 %psum.36 = f32[512]{0:T(512)S(1)} all-reduce(f32[512]{0:T(512)S(1)} %multiply_reduce_fusion), channel_id=1, replica_groups=mesh['grp'=4,'row_0'=8,'row_1'=2,'col'=16] {'grp'}, use_global_device_ids=true, to_apply=%region_14.15 | all-reduce | flops 512 | bytes 4096 | tf_op jit(solution)/shard_map/psum | solution.py:67
  675.9 10.9 %psum.37 = f32[512]{0:T(512)S(1)} all-reduce(f32[512]{0:T(512)S(1)} %psum.36), channel_id=1, replica_groups=mesh['grp'=4,'row_0'=8,'row_1'=2,'col'=16] {'row_0'}, use_global_device_ids=true, to_apply=%region_15.16 | all-reduce | flops 512 | bytes 4096 | tf_op jit(solution)/shard_map/psum | solution.py:67
  686.7 7.9 psum.38
  694.6 25.3 %psum.39 = f32[512]{0:T(512)S(1)} all-reduce(f32[512]{0:T(512)S(1)} %psum.38), channel_id=1, replica_groups=mesh['grp'=4,'row_0'=8,'row_1'=2,'col'=16] {'col'}, use_global_device_ids=true, to_apply=%region_17.18 | all-reduce | flops 512 | bytes 4096 | tf_op jit(solution)/shard_map/psum | solution.py:67
  724.7 89.3 %all-gather.4.cloned.1.call-done = bf16[1536,512]{1,0:T(8,128)(2,1)} async-done(((bf16[24,512]{1,0:T(8,128)(2,1)}), bf16[1536,512]{1,0:T(8,128)(2,1)}) %all-gather.4.cloned.1.call-update) | async-done | bytes 1572880 | tf_op jit(solution)/shard_map/all_gather | solution.py:101
  (97 shorter events, 51.6 us)
Async XLA Ops:
  7.2 1.4 copy-start
  7.2 283.5 %all-reduce.3.cloned.1.call-start = ((), (), s32[]{:S(2)}) async-start(), calls=%async_computation.3 | async-start | bytes 786432 | tf_op jit(solution)/shard_map/psum | solution.py:78
  11.3 329.9 %reduce-scatter.3.cloned.1.call-start = ((), (), s32[]{:S(2)}) async-start(), calls=%async_computation.4 | async-start | bytes 1179648 | tf_op jit(solution)/shard_map/reduce_scatter | solution.py:32
  293.9 78.7 %reduce-scatter.5.cloned.1.call-start = ((), (), s32[]{:S(2)}) async-start(), calls=%async_computation.5 | async-start | bytes 196608 | tf_op jit(solution)/shard_map/reduce_scatter | solution.py:32
  341.1 74.9 %all-gather.6.cloned.1.call-start = ((), (), s32[]{:S(2)}) async-start(), calls=%async_computation.7 | async-start | bytes 1179648 | tf_op jit(solution)/shard_map/all_gather | solution.py:39
  376.0 438.0 %all-gather.4.cloned.1.call-start = ((), (), s32[]{:S(2)}) async-start(), calls=%async_computation.6 | async-start | bytes 1597440 | tf_op jit(solution)/shard_map/all_gather | solution.py:101
  425.6 1.0 copy-start.4
  567.4 0.7 copy-start.7
  569.3 7.3 copy-start.1
  569.3 7.3 copy-start.3
  574.1 3.2 copy-start.5
  576.6 0.6 copy-start.6
  816.4 1.7 copy-start.2
Sparse Core Ops, SparseCore 0:
  12.0 278.6 all-reduce.2
  294.7 46.4 reduce-scatter.2
  344.5 28.1 reduce-scatter.4
  376.1 39.9 all-gather.5
  721.5 92.3 all-gather.3
where the time goes:
time: 827 us; the launch traced here: 826 us
  waiting for transfers between devices  487 us (59%)
  blocking collectives  142 us (17%)
  other arithmetic  134 us (16%)
  matrix products  23.2 us (3%)
  local copies, waits for them, and re-layouts  21.3 us (3%)
  between operations  17.4 us (2%)
    psum x1, waiting for transfers between devices, per_device(): left_factor = lax.psum(left_factor, ('grp', 'col'))  279 us
    all_gather x1, waiting for transfers between devices, per_device(): new_basis = lax.all_gather(basis_piece, GRP_ROW, axis=0, tiled=True)  89.3 us
    all_to_all x1, blocking collectives, sent_and_summed(): lax.all_to_all(tiles, axis, split_axis=0, concat_axis=0, tiled=True)  86.3 us
    another operation x14, other arithmetic, per_device(): cholesky_factor = jnp.linalg.cholesky(shifted)  78.7 us
    reduce_scatter x2, waiting for transfers between devices, reduced_to_own(): tiles = lax.psum_scatter(tiles, axes[k], scatter_dimension=0, tiled=True)  78.6 us
    psum x4, blocking collectives, by_axis(): shard = lax.psum(shard, axis)  52.8 us
    another operation x3, other arithmetic, per_device(): jax.scipy.linalg.solve_triangular(cholesky_factor, left_factor.T, lower=T...  40.4 us
    all_gather x1, waiting for transfers between devices, gather_in_order(): tiles = lax.all_gather(tiles, axes[k])  40 us
  transfers between devices with their start and end apart: 5, of which 5 were waited for; matrix products, arithmetic and copies ran while one was open for 0% of the time, Pallas kernels for 0%

commit v1 on v0

v1 whole, which is shorter than its diff:
```python
import functools
import math

import jax
import jax.numpy as jnp
from jax import lax
from jax.experimental import pallas as pl
from jax.experimental.pallas import tpu as pltpu
from jax.sharding import Mesh
from jax.sharding import PartitionSpec as P

MESH = pl.DeviceIdType.MESH
X, Y, K, Z = "grp", "row_0", "row_1", "col"
ROW = (Y, K)

momentum_decay = 0.9
ridge_scale = 0.0001
epsilon = 1e-06


def peer_of(axis, offset):
    return lax.rem(lax.axis_index(axis) + offset, lax.axis_size(axis))


def meet(axes):
    barrier = pltpu.get_barrier_semaphore()
    count = 0
    for axis in axes:
        for j in range(1, lax.axis_size(axis)):
            pl.semaphore_signal(barrier, inc=1, device_id={axis: peer_of(axis, j)}, device_id_type=MESH)
            count += 1
    return lambda: pl.semaphore_wait(barrier, count)


def send(src, dst, send_sem, recv_sem, axis, peer):
    copy = pltpu.make_async_remote_copy(
        src_ref=src, dst_ref=dst, send_sem=send_sem, recv_sem=recv_sem,
        device_id={axis: peer}, device_id_type=MESH,
    )
    copy.start()
    return copy


def scatter(tiles, arrived, sems, axis):
    copies = []
    for j in range(1, lax.axis_size(axis)):
        peer = peer_of(axis, j)
        copies.append(send(tiles.at[peer], arrived.at[j - 1], sems.at[0, j - 1], sems.at[1, j - 1], axis, peer))
    return copies


def share(slot, sems, axis):
    return [
        send(slot, slot, sems.at[0, j - 1], sems.at[1, j - 1], axis, peer_of(axis, j))
        for j in range(1, lax.axis_size(axis))
    ]


def arrive(copies):
    for copy in copies:
        copy.wait_recv()


def depart(copies):
    for copy in copies:
        copy.wait_send()


def left_kernel(
    mom, grad, basis, gram, left, low, part, xin, zpart, zin, lall, gall, gpair, kin, yall, gfull,
    sx, sz, sza, sxa, sk, sy, sgz, sgx, sgk,
):
    nx, ny, nz = lax.axis_size(X), lax.axis_size(Y), lax.axis_size(Z)
    g, y, k, c = (lax.axis_index(a) for a in (X, Y, K, Z))
    gathered = meet((X, Y, K, Z))
    rows = mom.shape[0]
    lanes = part.shape[2]
    fours = zpart.shape[1]
    merged_low = (mom[...] + grad[...].astype(jnp.float32)).astype(jnp.bfloat16)
    low[...] = merged_low
    product = jnp.dot(merged_low, basis[...], preferred_element_type=jnp.float32)
    for b in range(nx):
        part[b] = product[:, b * lanes : (b + 1) * lanes]
    gathered()
    sent = scatter(part, xin, sx, X)
    pending = list(sent)
    arrive(sent)
    total = part[g]
    for j in range(nx - 1):
        total = total + xin[j]
    for q in range(rows // 4):
        zpart[q // fours, q % fours] = total[4 * q : 4 * q + 4]
    sent = scatter(zpart, zin, sz, Z)
    pending += sent
    arrive(sent)
    own = zpart[c]
    for j in range(nz - 1):
        own = own + zin[j]
    lall[g, c] = own
    sent = share(lall.at[g, c], sza, Z)
    pending += sent
    arrive(sent)
    sent = share(lall.at[g], sxa, X)
    pending += sent
    arrive(sent)
    for b in range(nx):
        for q in range(rows // 4):
            left[4 * q : 4 * q + 4, b * lanes : (b + 1) * lanes] = lall[b, q // fours, q % fours]
    mine = left[:, pl.ds(pl.multiple_of(g * lanes, lanes), lanes)]
    gall[...] = lax.dot_general(
        mine, left[...], (((0,), (0,)), ((), ())),
        precision=lax.Precision.HIGHEST, preferred_element_type=jnp.float32,
    )
    strip = gall[pl.ds(pl.multiple_of(c * 8, 8), 8), :]
    half = strip.shape[1] // 2
    gpair[0] = strip[:, :half]
    gpair[1] = strip[:, half:]
    sent = scatter(gpair, kin, sk, K)
    pending += sent
    arrive(sent)
    yall[y] = gpair[k] + kin[0]
    sent = share(yall.at[y], sy, Y)
    pending += sent
    arrive(sent)
    total = yall[0]
    for j in range(1, ny):
        total = total + yall[j]
    gfull[k, g, c] = total
    sent = share(gfull.at[k, g, c], sgz, Z)
    pending += sent
    arrive(sent)
    sent = share(gfull.at[k, g], sgx, X)
    pending += sent
    arrive(sent)
    sent = share(gfull.at[k], sgk, K)
    pending += sent
    arrive(sent)
    for h in range(2):
        for b in range(nx):
            for q in range(nz):
                at = (b * nz + q) * 8
                gram[at : at + 8, h * half : (h + 1) * half] = gfull[h, b, q]
    depart(pending)


def left_call(mom, grad, basis):
    nx, ny, nz = lax.axis_size(X), lax.axis_size(Y), lax.axis_size(Z)
    rows, cols = mom.shape
    rank = basis.shape[1]
    lanes = rank // nx
    fours = rows // nz // 4
    half = rank // 2
    f32 = jnp.float32
    dma = lambda n: pltpu.SemaphoreType.DMA((2, n - 1))
    vmem = pl.BlockSpec(memory_space=pltpu.VMEM)
    return pl.pallas_call(
        left_kernel,
        out_shape=(
            jax.ShapeDtypeStruct((rank, rank), f32),
            jax.ShapeDtypeStruct((rows, rank), f32),
            jax.ShapeDtypeStruct((rows, cols), jnp.bfloat16),
        ),
        in_specs=[vmem] * 3,
        out_specs=(vmem,) * 3,
        scratch_shapes=[
            pltpu.VMEM((nx, rows, lanes), f32),
            pltpu.VMEM((nx - 1, rows, lanes), f32),
            pltpu.VMEM((nz, fours, 4, lanes), f32),
            pltpu.VMEM((nz - 1, fours, 4, lanes), f32),
            pltpu.VMEM((nx, nz, fours, 4, lanes), f32),
            pltpu.VMEM((lanes, rank), f32),
            pltpu.VMEM((2, 8, half), f32),
            pltpu.VMEM((1, 8, half), f32),
            pltpu.VMEM((ny, 8, half), f32),
            pltpu.VMEM((2, nx, nz, 8, half), f32),
            dma(nx), dma(nz), dma(nz), dma(nx), dma(2), dma(ny), dma(nz), dma(nx), dma(2),
        ],
        compiler_params=pltpu.CompilerParams(collective_id=0, has_side_effects=True),
        name="left",
    )(mom, grad, basis)


def right_kernel(
    groups, whole_rows, update_scale,
    mom, grad, low, orth, newmom, basis_out, update, ksend, kin, mine, xsend, xin, ysum, ysend, yin, nb, stack,
    qz, qk, qx, qy, sk, sx, sy, say, sax, sak, sqz, sqk, sqx, sqy,
):
    nx, ny, nz = lax.axis_size(X), lax.axis_size(Y), lax.axis_size(Z)
    g, y, k, c = (lax.axis_index(a) for a in (X, Y, K, Z))
    gathered = meet((X, Y, K, Z))
    rows, cols = mom.shape
    rank = orth.shape[1]
    half = cols // 2
    f32, bf16 = jnp.float32, jnp.bfloat16
    stack[:rows] = orth[...].astype(bf16)

    def product(at):
        return lax.dot_general(
            low[:, pl.ds(pl.multiple_of(at, 128), 128)], stack[:rows], (((0,), (0,)), ((), ())),
            preferred_element_type=f32,
        ) * (1.0 / groups)

    @pl.loop(0, half // 128)
    def _(i):
        ksend[pl.ds(pl.multiple_of(i * 128, 128), 128), :] = product((1 - k) * half + i * 128).astype(bf16)

    gathered()
    sent = [send(ksend, kin, sk.at[0, 0], sk.at[1, 0], K, 1 - k)]
    pending = list(sent)

    @pl.loop(0, half // 128)
    def _(i):
        mine[pl.ds(pl.multiple_of(i * 128, 128), 128), :] = product(k * half + i * 128)

    arrive(sent)
    block = half // nx
    for b in range(nx):
        at = slice(b * block, (b + 1) * block)
        both = mine[at] + kin[at].astype(f32)
        mine[at] = both
        xsend[b] = both.astype(bf16)
    sent = scatter(xsend, xin, sx, X)
    pending += sent
    arrive(sent)
    total = mine[pl.ds(pl.multiple_of(g * block, block), block), :]
    for j in range(nx - 1):
        total = total + xin[j].astype(f32)
    ysum[...] = total
    piece_rows = block // ny
    for b in range(ny):
        ysend[b] = total[b * piece_rows : (b + 1) * piece_rows].astype(bf16)
    sent = scatter(ysend, yin, sy, Y)
    pending += sent
    arrive(sent)
    piece = ysum[pl.ds(pl.multiple_of(y * piece_rows, 8), piece_rows), :]
    for j in range(ny - 1):
        piece = piece + yin[j].astype(f32)
    nb[k, g, y] = piece.astype(bf16)
    qz[c] = jnp.sum(piece * piece, axis=0, keepdims=True)
    sent_z = share(qz.at[c], sqz, Z)
    sent_y = share(nb.at[k, g, y], say, Y)
    pending += sent_z + sent_y

    def summed(ref, n):
        acc = ref[0]
        for j in range(1, n):
            acc = acc + ref[j]
        return acc

    arrive(sent_z)
    qk[k] = summed(qz, nz)
    sent = share(qk.at[k], sqk, K)
    pending += sent
    arrive(sent)
    qx[g] = summed(qk, 2)
    sent = share(qx.at[g], sqx, X)
    pending += sent
    arrive(sent_y)
    sent_x = share(nb.at[k, g], sax, X)
    pending += sent_x
    arrive(sent)
    qy[y] = summed(qx, nx)
    sent = share(qy.at[y], sqy, Y)
    pending += sent
    arrive(sent)
    squares = summed(qy, ny)
    column_rms = jnp.sqrt(squares / whole_rows + epsilon)
    inverse = 1.0 / column_rms
    stack[rows:] = (orth[...] * column_rms).astype(bf16)
    arrive(sent_x)
    sent = share(nb.at[k], sak, K)
    pending += sent
    arrive(sent)
    for h in range(2):
        for b in range(nx):
            for p in range(ny):
                at = h * half + b * block + p * piece_rows
                basis_out[at : at + piece_rows] = (nb[h, b, p].astype(f32) * inverse).astype(bf16)

    @pl.loop(0, cols // 256)
    def _(i):
        at = pl.ds(pl.multiple_of(i * 256, 256), 256)
        both = lax.dot_general(stack[...], basis_out[at, :], (((1,), (1,)), ((), ())), preferred_element_type=f32)
        update[:, at] = (update_scale * both[:rows]).astype(bf16)
        newmom[:, at] = mom[:, at] + grad[:, at].astype(f32) - (1 - momentum_decay) * both[rows:]

    depart(pending)


def right_call(mom, grad, low, orth, update_scale):
    nx, ny, nz = lax.axis_size(X), lax.axis_size(Y), lax.axis_size(Z)
    rows, cols = mom.shape
    rank = orth.shape[1]
    half = cols // 2
    block = half // nx
    piece = block // ny
    f32, bf16 = jnp.float32, jnp.bfloat16
    dma = lambda n: pltpu.SemaphoreType.DMA((2, n - 1))
    vmem = pl.BlockSpec(memory_space=pltpu.VMEM)
    return pl.pallas_call(
        functools.partial(right_kernel, nx, cols * nz, update_scale),
        out_shape=(
            jax.ShapeDtypeStruct((rows, cols), f32),
            jax.ShapeDtypeStruct((cols, rank), bf16),
            jax.ShapeDtypeStruct((rows, cols), bf16),
        ),
        in_specs=[vmem] * 4,
        out_specs=(vmem,) * 3,
        scratch_shapes=[
            pltpu.VMEM((half, rank), bf16),
            pltpu.VMEM((half, rank), bf16),
            pltpu.VMEM((half, rank), f32),
            pltpu.VMEM((nx, block, rank), bf16),
            pltpu.VMEM((nx - 1, block, rank), bf16),
            pltpu.VMEM((block, rank), f32),
            pltpu.VMEM((ny, piece, rank), bf16),
            pltpu.VMEM((ny - 1, piece, rank), bf16),
            pltpu.VMEM((2, nx, ny, piece, rank), bf16),
            pltpu.VMEM((2 * rows, rank), bf16),
            pltpu.VMEM((nz, 1, rank), f32),
            pltpu.VMEM((2, 1, rank), f32),
            pltpu.VMEM((nx, 1, rank), f32),
            pltpu.VMEM((ny, 1, rank), f32),
            dma(2), dma(nx), dma(ny), dma(ny), dma(nx), dma(2), dma(nz), dma(2), dma(nx), dma(ny),
        ],
        compiler_params=pltpu.CompilerParams(collective_id=1, has_side_effects=True),
        name="right",
    )(mom, grad, low, orth)


def factor_kernel(gram, left, orth, a, diag):
    f32 = jnp.float32
    rank = gram.shape[0]
    rows = left.shape[0]
    size = 128
    sub = lax.broadcasted_iota(jnp.int32, (8, size), 0)
    lane = lax.broadcasted_iota(jnp.int32, (8, size), 1)
    at_row = lax.broadcasted_iota(jnp.int32, (size, size), 0)
    at_col = lax.broadcasted_iota(jnp.int32, (size, size), 1)
    trace = jnp.zeros((size, size), f32)
    for b in range(rank // size):
        s = slice(b * size, (b + 1) * size)
        trace = trace + jnp.where(at_row == at_col, gram[s, s], 0.0)
    shift = ridge_scale * (jnp.sum(trace) / rank)
    a[:rank] = gram[...]
    for b in range(rank // size):
        s = slice(b * size, (b + 1) * size)
        a[s, s] = gram[s, s] + jnp.where(at_row == at_col, shift, 0.0)
    a[rank:] = left[...]

    def spread(v, l):
        return jnp.broadcast_to(v[:, l : l + 1], (8, size))

    def everywhere(v, i):
        return jnp.broadcast_to(v[i : i + 1, :], (8, size))

    def folded(v):
        return jnp.broadcast_to(jnp.sum(v, axis=0, keepdims=True), (8, size))

    def packed(lines):
        out = lines[0]
        for i in range(1, 8):
            out = jnp.where(sub == i, lines[i], out)
        return out

    def dot(x, y):
        return lax.dot_general(
            x, y, (((1,), (1,)), ((), ())), precision=lax.Precision.HIGHEST, preferred_element_type=f32
        )

    @pl.loop(0, rank // size)
    def _(block):
        off = pl.multiple_of(block * size, size)
        diag[0] = a[pl.ds(off, size), pl.ds(off, size)]
        upper, inverse = [], []
        for s in range(size // 8):
            base = 8 * s
            lines, other = [], []
            for i in range(8):
                line = jnp.broadcast_to(diag[0, base + i : base + i + 1, :], (8, size))
                unit = jnp.where(lane == base + i, 1.0, 0.0)
                if s:
                    acc_u = acc_w = None
                    for t in range(s):
                        factor = spread(upper[t], base + i)
                        u, w = factor * upper[t], factor * inverse[t]
                        acc_u = u if acc_u is None else acc_u + u
                        acc_w = w if acc_w is None else acc_w + w
                    line = line - folded(acc_u)
                    unit = unit - folded(acc_w)
                lines.append(line)
                other.append(unit)
            panel = packed(lines)
            cols = [spread(panel, base + j) for j in range(8)]
            d = [[everywhere(cols[j], i) if j >= i else None for j in range(8)] for i in range(8)]
            for j in range(8):
                scale = lax.rsqrt(d[j][j])
                lines[j] = lines[j] * scale
                other[j] = other[j] * scale
                u = [None] * 8
                for i in range(j + 1, 8):
                    u[i] = d[j][i] * scale
                for i in range(j + 1, 8):
                    for m in range(i, 8):
                        d[i][m] = d[i][m] - u[i] * u[m]
                for i in range(j + 1, 8):
                    lines[i] = lines[i] - u[i] * lines[j]
                    other[i] = other[i] - u[i] * other[j]
            upper.append(packed(lines))
            inverse.append(packed(other))
            diag[1, base : base + 8, :] = inverse[s]
        for b in range(rank // size):

            @pl.when(block == b)
            def _():
                at, after = b * size, (b + 1) * size
                below = dot(a[after:, at:after], diag[1])
                a[after:, at:after] = below
                if after < rank:
                    a[after:, after:] = a[after:, after:] - dot(below, below[: rank - after])

    orth[...] = a[rank:]


def factor_call(gram, left):
    rank, rows = gram.shape[0], left.shape[0]
    vmem = pl.BlockSpec(memory_space=pltpu.VMEM)
    return pl.pallas_call(
        factor_kernel,
        out_shape=jax.ShapeDtypeStruct((rows, rank), jnp.float32),
        in_specs=[vmem] * 2,
        out_specs=vmem,
        scratch_shapes=[pltpu.VMEM((rank + rows, rank), jnp.float32), pltpu.VMEM((2, 128, 128), jnp.float32)],
        name="factor",
    )(gram, left)


def per_device(gradients, momentum, right_basis):
    mom, grad = momentum[0], gradients[0]
    rank = right_basis.shape[1]
    whole_rows = mom.shape[0] * lax.axis_size(Y) * lax.axis_size(K)
    gram_matrix, left_factor, merged_low = left_call(mom, grad, right_basis)
    orthonormal = factor_call(gram_matrix, left_factor)
    new_momentum, new_basis, update = right_call(
        mom, grad, merged_low, orthonormal, math.sqrt(whole_rows / rank)
    )
    return new_momentum[None], new_basis, update


def solution(mesh):
    torus = Mesh(
        mesh.devices.reshape(mesh.shape["grp"], mesh.shape["row"] // 2, 2, mesh.shape["col"]),
        (X, Y, K, Z),
    )
    return jax.shard_map(
        per_device,
        mesh=torus,
        in_specs=(P(X, ROW, Z), P(X, ROW, Z), P(Z, None)),
        out_specs=(P(X, ROW, Z), P(Z, None), P(ROW, Z)),
        check_vma=False,
    )
```

time: 827 us -> 168 us (0.20)
  waiting for transfers between devices: 487 us -> 0 us
  Pallas kernels: 0 us -> 162 us
  blocking collectives: 142 us -> 0 us
  other arithmetic: 134 us -> 0 us
  matrix products: 23.2 us -> 0 us
  between operations: 17.4 us -> 0.66 us
  local copies, waits for them, and re-layouts: 21.3 us -> 4.76 us
    psum x1 -> x0, waiting for transfers between devices: 279 us -> none  [per_device(): left_factor = lax.psum(left_factor, ('grp', 'col'))]
    pallas_call x0 -> x3, Pallas kernels: none -> 162 us  [the longest x1 83.1 us: left_call(): pl.pallas_call(left_kernel, out_shape=(jax.ShapeDtypeStruct((rank, rank),...]
    all_gather x2 -> x0, waiting for transfers between devices: 129 us -> none  [the longest x1 89.3 us: per_device(): new_basis = lax.all_gather(basis_piece, GRP_ROW, axis=0, tiled=True)]
    another operation x17 -> x0, other arithmetic: 119 us -> none  [the longest x14 78.7 us: per_device(): cholesky_factor = jnp.linalg.cholesky(shifted)]
    all_to_all x1 -> x0, blocking collectives: 86.3 us -> none  [sent_and_summed(): lax.all_to_all(tiles, axis, split_axis=0, concat_axis=0, tiled=True)]
    reduce_scatter x2 -> x0, waiting for transfers between devices: 78.6 us -> none  [reduced_to_own(): tiles = lax.psum_scatter(tiles, axes[k], scatter_dimension=0, tiled=True)]
    psum x4 -> x0, blocking collectives: 52.8 us -> none  [by_axis(): shard = lax.psum(shard, axis)]
    another operation x35 -> x0, local copies, waits for them, and re-layouts: 14.6 us -> none
  transfers between devices with their start and end apart: 5 -> 0, of which waited for: 5 -> 0; matrix products, arithmetic and copies ran while one was open for 0% -> 0% of each run, Pallas kernels for 0% -> 0%
where the time goes in v1:
time: 168 us; the launch traced here: 167 us
  Pallas kernels  162 us (96%)
  local copies, waits for them, and re-layouts  4.76 us (3%)
    pallas_call x1, Pallas kernels, left_call(): pl.pallas_call(left_kernel, out_shape=(jax.ShapeDtypeStruct((rank, rank),...  83.1 us
    pallas_call x1, Pallas kernels, right_call(): pl.pallas_call(functools.partial(right_kernel, nx, cols * nz, update_scal...  55 us
    pallas_call x1, Pallas kernels, factor_call(): pl.pallas_call(factor_kernel, out_shape=jax.ShapeDtypeStruct((rows, rank)...  23.7 us
    unnamed x7, local copies, waits for them, and re-layouts  4.76 us

profile of v1, /device:TPU:1, one launch (start us, length us, event | category | flops | bytes accessed | tf_op | source)
XLA Modules:
  0.0 167.2 jit_solution(862542122023225722)
XLA Ops:
  0.6 83.1 %left.1 = (f32[512,512]{1,0:T(8,128)}, f32[192,512]{1,0:T(8,128)}, bf16[192,1536]{1,0:T(8,128)(2,1)}) custom-call(f32[192,1536]{1,0:T(8,128)} %bitcast.3, bf16[192,1536]{1,0:T(8,128)(2,1)} %bitcast.5, bf16[1536,512]{1,0:T(8,128)(2,1)} %basis.1), custom_call_target="tpu_custom_call" | custom-call | tf_op jit(solution)/shard_map/left/pallas_call | solution.py:156
  83.7 23.7 %factor.1.orth = f32[192,512]{1,0:T(8,128)} custom-call(f32[512,512]{1,0:T(8,128)} %get-tuple-element.10.gram, f32[192,512]{1,0:T(8,128)} %get-tuple-element.11.left), custom_call_target="tpu_custom_call" | custom-call | tf_op jit(solution)/shard_map/factor/pallas_call | solution.py:428
  107.5 55.0 %right.1 = (f32[192,1536]{1,0:T(8,128)}, bf16[1536,512]{1,0:T(8,128)(2,1)}, bf16[192,1536]{1,0:T(8,128)(2,1)}) custom-call(f32[192,1536]{1,0:T(8,128)} %bitcast.4, bf16[192,1536]{1,0:T(8,128)(2,1)} %bitcast.6, bf16[192,1536]{1,0:T(8,128)(2,1)} %get-tuple-element.9.low, f32[192,512]{1,0:T(8,128)} %factor.1.orth), custom_call_target="tpu_custom_call" | custom-call | tf_op jit(solution)/shard_map/right/pallas_call | solution.py:300
  162.4 0.0 copy-start
  162.5 2.5 %copy.9 = f32[1,192,1536]{2,1,0:T(8,128)} copy(f32[1,192,1536]{2,1,0:T(8,128)} %bitcast.7) | data formatting | bytes 2359296
  164.9 0.0 copy-done
  164.9 0.0 copy-start.1
  164.9 1.1 copy.10
  166.1 0.3 copy-done.1
  166.4 0.8 copy.11
Async XLA Ops:
  162.4 2.5 %copy-start = (bf16[1536,512]{1,0:T(8,128)(2,1)S(1)}, bf16[1536,512]{1,0:T(8,128)(2,1)}, u32[]{:S(2)}) copy-start(bf16[1536,512]{1,0:T(8,128)(2,1)} %get-tuple-element.19) | copy-start | bytes 4718596
  164.9 1.5 copy-start.1

commit v2 on v1

v2 whole, which is shorter than its diff:
```python
import functools
import math

import jax
import jax.numpy as jnp
from jax import lax
from jax.experimental import pallas as pl
from jax.experimental.pallas import tpu as pltpu
from jax.sharding import Mesh
from jax.sharding import PartitionSpec as P

MESH = pl.DeviceIdType.MESH
X, Y, K, Z = "grp", "row_0", "row_1", "col"
ROW = (Y, K)

momentum_decay = 0.9
ridge_scale = 0.0001
epsilon = 1e-06


def peer_of(axis, offset):
    return lax.rem(lax.axis_index(axis) + offset, lax.axis_size(axis))


def meet(axes):
    barrier = pltpu.get_barrier_semaphore()
    count = 0
    for axis in axes:
        for j in range(1, lax.axis_size(axis)):
            pl.semaphore_signal(barrier, inc=1, device_id={axis: peer_of(axis, j)}, device_id_type=MESH)
            count += 1
    return lambda: pl.semaphore_wait(barrier, count)


def send(src, dst, send_sem, recv_sem, axis, peer):
    copy = pltpu.make_async_remote_copy(
        src_ref=src, dst_ref=dst, send_sem=send_sem, recv_sem=recv_sem,
        device_id={axis: peer}, device_id_type=MESH,
    )
    copy.start()
    return copy


def scatter(tiles, arrived, sems, axis):
    copies = []
    for j in range(1, lax.axis_size(axis)):
        peer = peer_of(axis, j)
        copies.append(send(tiles.at[peer], arrived.at[j - 1], sems.at[0, j - 1], sems.at[1, j - 1], axis, peer))
    return copies


def share(slot, sems, axis):
    return [
        send(slot, slot, sems.at[0, j - 1], sems.at[1, j - 1], axis, peer_of(axis, j))
        for j in range(1, lax.axis_size(axis))
    ]


def arrive(copies):
    for copy in copies:
        copy.wait_recv()


def depart(copies):
    for copy in copies:
        copy.wait_send()


def left_kernel(
    mom, grad, basis, gram, left, low, part, xin, zpart, zin, lall, gall, gpair, kin, yall, gfull,
    sx, sz, sza, sxa, sk, sy, sgz, sgx, sgk,
):
    nx, ny, nz = lax.axis_size(X), lax.axis_size(Y), lax.axis_size(Z)
    g, y, k, c = (lax.axis_index(a) for a in (X, Y, K, Z))
    gathered = meet((X, Y, K, Z))
    chunks, lanes = part.shape[0], part.shape[3]
    tall = 4 * nz
    merged_low = (mom[...] + grad[...].astype(jnp.float32)).astype(jnp.bfloat16)
    low[...] = merged_low
    product = jnp.dot(merged_low, basis[...], preferred_element_type=jnp.float32)
    for t in range(chunks):
        for b in range(nx):
            part[t, b] = product[t * tall : (t + 1) * tall, b * lanes : (b + 1) * lanes]
    gathered()
    pending = []

    def started(copies):
        pending.extend(copies)
        return copies

    sent = [started(scatter(part.at[t], xin.at[t], sx.at[t], X)) for t in range(chunks)]
    after = []
    for t in range(chunks):
        arrive(sent[t])
        total = part[t, g]
        for j in range(nx - 1):
            total = total + xin[t, j]
        for q in range(nz):
            zpart[t, q] = total[4 * q : 4 * q + 4]
        after.append(started(scatter(zpart.at[t], zin.at[t], sz.at[t], Z)))
    sent, after = after, []
    for t in range(chunks):
        arrive(sent[t])
        own = zpart[t, c]
        for j in range(nz - 1):
            own = own + zin[t, j]
        lall[t, g, c] = own
        after.append(started(share(lall.at[t, g, c], sza.at[t], Z)))
    sent, after = after, []
    for t in range(chunks):
        arrive(sent[t])
        after.append(started(share(lall.at[t, g], sxa.at[t], X)))
    for t in range(chunks):
        arrive(after[t])
        rows = slice(t * tall, (t + 1) * tall)
        for b in range(nx):
            for q in range(nz):
                left[t * tall + 4 * q : t * tall + 4 * q + 4, b * lanes : (b + 1) * lanes] = lall[t, b, q]
        mine = left[rows, pl.ds(pl.multiple_of(g * lanes, lanes), lanes)]
        outer = lax.dot_general(
            mine, left[rows, :], (((0,), (0,)), ((), ())),
            precision=lax.Precision.HIGHEST, preferred_element_type=jnp.float32,
        )
        gall[...] = outer if t == 0 else gall[...] + outer
    strip = gall[pl.ds(pl.multiple_of(c * 8, 8), 8), :]
    half = strip.shape[1] // 2
    gpair[0] = strip[:, :half]
    gpair[1] = strip[:, half:]
    sent = started(scatter(gpair, kin, sk, K))
    arrive(sent)
    yall[y] = gpair[k] + kin[0]
    sent = started(share(yall.at[y], sy, Y))
    arrive(sent)
    total = yall[0]
    for j in range(1, ny):
        total = total + yall[j]
    parts = gfull.shape[1]
    wide = half // parts
    sent = []
    for u in range(parts):
        gfull[k, u, g, c] = total[:, u * wide : (u + 1) * wide]
        sent.append(started(share(gfull.at[k, u, g, c], sgz.at[u], Z)))
    after = []
    for u in range(parts):
        arrive(sent[u])
        after.append(started(share(gfull.at[k, u, g], sgx.at[u], X)))
    sent = []
    for u in range(parts):
        arrive(after[u])
        sent.append(started(share(gfull.at[k, u], sgk.at[u], K)))
    for u in range(parts):
        arrive(sent[u])
    for h in range(2):
        for u in range(parts):
            for b in range(nx):
                for q in range(nz):
                    at = (b * nz + q) * 8
                    lane = h * half + u * wide
                    gram[at : at + 8, lane : lane + wide] = gfull[h, u, b, q]
    depart(pending)


def copies_of(count, n):
    return pltpu.SemaphoreType.DMA((count, 2, n - 1) if count else (2, n - 1))


def left_call(mom, grad, basis):
    nx, ny, nz = lax.axis_size(X), lax.axis_size(Y), lax.axis_size(Z)
    rows, cols = mom.shape
    rank = basis.shape[1]
    lanes = rank // nx
    chunks = rows // (4 * nz)
    half = rank // 2
    f32 = jnp.float32
    vmem = pl.BlockSpec(memory_space=pltpu.VMEM)
    return pl.pallas_call(
        left_kernel,
        out_shape=(
            jax.ShapeDtypeStruct((rank, rank), f32),
            jax.ShapeDtypeStruct((rows, rank), f32),
            jax.ShapeDtypeStruct((rows, cols), jnp.bfloat16),
        ),
        in_specs=[vmem] * 3,
        out_specs=(vmem,) * 3,
        scratch_shapes=[
            pltpu.VMEM((chunks, nx, 4 * nz, lanes), f32),
            pltpu.VMEM((chunks, nx - 1, 4 * nz, lanes), f32),
            pltpu.VMEM((chunks, nz, 4, lanes), f32),
            pltpu.VMEM((chunks, nz - 1, 4, lanes), f32),
            pltpu.VMEM((chunks, nx, nz, 4, lanes), f32),
            pltpu.VMEM((lanes, rank), f32),
            pltpu.VMEM((2, 8, half), f32),
            pltpu.VMEM((1, 8, half), f32),
            pltpu.VMEM((ny, 8, half), f32),
            pltpu.VMEM((2, 2, nx, nz, 8, half // 2), f32),
            copies_of(chunks, nx), copies_of(chunks, nz), copies_of(chunks, nz), copies_of(chunks, nx),
            copies_of(0, 2), copies_of(0, ny), copies_of(2, nz), copies_of(2, nx), copies_of(2, 2),
        ],
        compiler_params=pltpu.CompilerParams(collective_id=0, has_side_effects=True),
        name="left",
    )(mom, grad, basis)


def right_kernel(
    groups, whole_rows, low, orth, nb_out, rms_out, ksend, kin, mine, xsend, xin, ysum, ysend, yin, nb, low_left,
    qz, qk, qx, qy, sk, sx, sy, say, sax, sak, sqz, sqk, sqx, sqy,
):
    nx, ny, nz = lax.axis_size(X), lax.axis_size(Y), lax.axis_size(Z)
    g, y, k, c = (lax.axis_index(a) for a in (X, Y, K, Z))
    gathered = meet((X, Y, K, Z))
    chunks, half, wide = ksend.shape
    f32, bf16 = jnp.float32, jnp.bfloat16
    low_left[...] = orth[...].astype(bf16)
    pending = []

    def started(copies):
        pending.extend(copies)
        return copies

    def product(at):
        return lax.dot_general(
            low[:, pl.ds(pl.multiple_of(at, 128), 128)], low_left[...], (((0,), (0,)), ((), ())),
            preferred_element_type=f32,
        ) * (1.0 / groups)

    @pl.loop(0, half // 128)
    def _(i):
        tile = product((1 - k) * half + i * 128).astype(bf16)
        for t in range(chunks):
            ksend[t, pl.ds(pl.multiple_of(i * 128, 128), 128), :] = tile[:, t * wide : (t + 1) * wide]

    gathered()
    sent = [
        started([send(ksend.at[t], kin.at[t], sk.at[t, 0, 0], sk.at[t, 1, 0], K, 1 - k)]) for t in range(chunks)
    ]

    @pl.loop(0, half // 128)
    def _(i):
        tile = product(k * half + i * 128)
        for t in range(chunks):
            mine[t, pl.ds(pl.multiple_of(i * 128, 128), 128), :] = tile[:, t * wide : (t + 1) * wide]

    block = half // nx
    piece_rows = block // ny
    after = []
    for t in range(chunks):
        arrive(sent[t])
        for b in range(nx):
            at = slice(b * block, (b + 1) * block)
            both = mine[t, at] + kin[t, at].astype(f32)
            mine[t, at] = both
            xsend[t, b] = both.astype(bf16)
        after.append(started(scatter(xsend.at[t], xin.at[t], sx.at[t], X)))
    sent, after = after, []
    for t in range(chunks):
        arrive(sent[t])
        total = mine[t, pl.ds(pl.multiple_of(g * block, block), block), :]
        for j in range(nx - 1):
            total = total + xin[t, j].astype(f32)
        ysum[t] = total
        for b in range(ny):
            ysend[t, b] = total[b * piece_rows : (b + 1) * piece_rows].astype(bf16)
        after.append(started(scatter(ysend.at[t], yin.at[t], sy.at[t], Y)))
    sent, after = after, []
    for t in range(chunks):
        arrive(sent[t])
        piece = ysum[t, pl.ds(pl.multiple_of(y * piece_rows, 8), piece_rows), :]
        for j in range(ny - 1):
            piece = piece + yin[t, j].astype(f32)
        nb[t, k, g, y] = piece.astype(bf16)
        qz[c, :, t * wide : (t + 1) * wide] = jnp.sum(piece * piece, axis=0, keepdims=True)
        if t == chunks - 1:
            sent_q = started(share(qz.at[c], sqz, Z))
        after.append(started(share(nb.at[t, k, g, y], say.at[t], Y)))

    def summed(ref, n):
        acc = ref[0]
        for j in range(1, n):
            acc = acc + ref[j]
        return acc

    sent, after = after, []
    for t in range(chunks):
        arrive(sent[t])
        after.append(started(share(nb.at[t, k, g], sax.at[t], X)))
    arrive(sent_q)
    qy[y] = summed(qz, nz)
    sent_q = started(share(qy.at[y], sqy, Y))
    sent = []
    for t in range(chunks - 1):
        arrive(after[t])
        sent.append(started(share(nb.at[t, k], sak.at[t], K)))
    arrive(sent_q)
    qx[g] = summed(qy, ny)
    sent_q = started(share(qx.at[g], sqx, X))
    arrive(after[-1])
    sent.append(started(share(nb.at[chunks - 1, k], sak.at[chunks - 1], K)))
    arrive(sent_q)
    qk[k] = summed(qx, nx)
    sent_q = started(share(qk.at[k], sqk, K))
    for t in range(chunks):
        arrive(sent[t])
        for h in range(2):
            for b in range(nx):
                for p in range(ny):
                    at = h * half + b * block + p * piece_rows
                    nb_out[t, at : at + piece_rows, :] = nb[t, h, b, p]
    arrive(sent_q)
    rms_out[...] = jnp.sqrt(summed(qk, 2) / whole_rows + epsilon)
    depart(pending)


def right_call(low, orth):
    nx, ny, nz = lax.axis_size(X), lax.axis_size(Y), lax.axis_size(Z)
    rows, cols = low.shape
    rank = orth.shape[1]
    half = cols // 2
    block = half // nx
    piece = block // ny
    wide = 128
    chunks = rank // wide
    f32, bf16 = jnp.float32, jnp.bfloat16
    vmem = pl.BlockSpec(memory_space=pltpu.VMEM)
    return pl.pallas_call(
        functools.partial(right_kernel, nx, cols * nz),
        out_shape=(
            jax.ShapeDtypeStruct((chunks, cols, wide), bf16),
            jax.ShapeDtypeStruct((1, rank), f32),
        ),
        in_specs=[vmem] * 2,
        out_specs=(vmem,) * 2,
        scratch_shapes=[
            pltpu.VMEM((chunks, half, wide), bf16),
            pltpu.VMEM((chunks, half, wide), bf16),
            pltpu.VMEM((chunks, half, wide), f32),
            pltpu.VMEM((chunks, nx, block, wide), bf16),
            pltpu.VMEM((chunks, nx - 1, block, wide), bf16),
            pltpu.VMEM((chunks, block, wide), f32),
            pltpu.VMEM((chunks, ny, piece, wide), bf16),
            pltpu.VMEM((chunks, ny - 1, piece, wide), bf16),
            pltpu.VMEM((chunks, 2, nx, ny, piece, wide), bf16),
            pltpu.VMEM((rows, rank), bf16),
            pltpu.VMEM((nz, 1, rank), f32),
            pltpu.VMEM((2, 1, rank), f32),
            pltpu.VMEM((nx, 1, rank), f32),
            pltpu.VMEM((ny, 1, rank), f32),
            copies_of(chunks, 2), copies_of(chunks, nx), copies_of(chunks, ny), copies_of(chunks, ny),
            copies_of(chunks, nx), copies_of(chunks, 2),
            copies_of(0, nz), copies_of(0, 2), copies_of(0, nx), copies_of(0, ny),
        ],
        compiler_params=pltpu.CompilerParams(collective_id=1, has_side_effects=True),
        name="right",
    )(low, orth)


def final_kernel(update_scale, nb, rms, orth, mom, grad, newmom, basis, update, stack):
    rows = mom.shape[0]
    chunks, wide = nb.shape[0], nb.shape[2]
    f32, bf16 = jnp.float32, jnp.bfloat16

    @pl.when(pl.program_id(0) == 0)
    def _():
        stack[:rows] = orth[...].astype(bf16)
        stack[rows:] = (orth[...] * rms[...]).astype(bf16)

    inverse = 1.0 / rms[...]
    for t in range(chunks):
        at = slice(t * wide, (t + 1) * wide)
        basis[:, at] = (nb[t].astype(f32) * inverse[:, at]).astype(bf16)
    both = lax.dot_general(stack[...], basis[...], (((1,), (1,)), ((), ())), preferred_element_type=f32)
    update[...] = (update_scale * both[:rows]).astype(bf16)
    newmom[...] = mom[...] + grad[...].astype(f32) - (1 - momentum_decay) * both[rows:]


def final_call(nb, rms, orth, mom, grad, update_scale):
    chunks, cols, wide = nb.shape
    rows, rank = orth.shape
    step = 512
    f32, bf16 = jnp.float32, jnp.bfloat16
    strip = pl.BlockSpec((rows, step), lambda i: (0, i))
    return pl.pallas_call(
        functools.partial(final_kernel, update_scale),
        grid=(cols // step,),
        out_shape=(
            jax.ShapeDtypeStruct((rows, cols), f32),
            jax.ShapeDtypeStruct((cols, rank), bf16),
            jax.ShapeDtypeStruct((rows, cols), bf16),
        ),
        in_specs=[
            pl.BlockSpec((chunks, step, wide), lambda i: (0, i, 0)),
            pl.BlockSpec((1, rank), lambda i: (0, 0)),
            pl.BlockSpec((rows, rank), lambda i: (0, 0)),
            strip,
            strip,
        ],
        out_specs=(strip, pl.BlockSpec((step, rank), lambda i: (i, 0)), strip),
        scratch_shapes=[pltpu.VMEM((2 * rows, rank), bf16)],
        name="final",
    )(nb, rms, orth, mom, grad)


def factor_kernel(gram, left, orth, a, diag):
    f32 = jnp.float32
    rank = gram.shape[0]
    rows = left.shape[0]
    size = 128
    sub = lax.broadcasted_iota(jnp.int32, (8, size), 0)
    lane = lax.broadcasted_iota(jnp.int32, (8, size), 1)
    at_row = lax.broadcasted_iota(jnp.int32, (size, size), 0)
    at_col = lax.broadcasted_iota(jnp.int32, (size, size), 1)
    trace = jnp.zeros((size, size), f32)
    for b in range(rank // size):
        s = slice(b * size, (b + 1) * size)
        trace = trace + jnp.where(at_row == at_col, gram[s, s], 0.0)
    shift = ridge_scale * (jnp.sum(trace) / rank)
    a[:rank] = gram[...]
    for b in range(rank // size):
        s = slice(b * size, (b + 1) * size)
        a[s, s] = gram[s, s] + jnp.where(at_row == at_col, shift, 0.0)
    a[rank:] = left[...]

    def spread(v, l):
        return jnp.broadcast_to(v[:, l : l + 1], (8, size))

    def everywhere(v, i):
        return jnp.broadcast_to(v[i : i + 1, :], (8, size))

    def folded(v):
        return jnp.broadcast_to(jnp.sum(v, axis=0, keepdims=True), (8, size))

    def packed(lines):
        out = lines[0]
        for i in range(1, 8):
            out = jnp.where(sub == i, lines[i], out)
        return out

    def dot(x, y):
        return lax.dot_general(
            x, y, (((1,), (1,)), ((), ())), precision=lax.Precision.HIGHEST, preferred_element_type=f32
        )

    @pl.loop(0, rank // size)
    def _(block):
        off = pl.multiple_of(block * size, size)
        diag[0] = a[pl.ds(off, size), pl.ds(off, size)]
        upper, inverse = [], []
        for s in range(size // 8):
            base = 8 * s
            lines, other = [], []
            for i in range(8):
                line = jnp.broadcast_to(diag[0, base + i : base + i + 1, :], (8, size))
                unit = jnp.where(lane == base + i, 1.0, 0.0)
                if s:
                    acc_u = acc_w = None
                    for t in range(s):
                        factor = spread(upper[t], base + i)
                        u, w = factor * upper[t], factor * inverse[t]
                        acc_u = u if acc_u is None else acc_u + u
                        acc_w = w if acc_w is None else acc_w + w
                    line = line - folded(acc_u)
                    unit = unit - folded(acc_w)
                lines.append(line)
                other.append(unit)
            panel = packed(lines)
            cols = [spread(panel, base + j) for j in range(8)]
            d = [[everywhere(cols[j], i) if j >= i else None for j in range(8)] for i in range(8)]
            for j in range(8):
                scale = lax.rsqrt(d[j][j])
                lines[j] = lines[j] * scale
                other[j] = other[j] * scale
                u = [None] * 8
                for i in range(j + 1, 8):
                    u[i] = d[j][i] * scale
                for i in range(j + 1, 8):
                    for m in range(i, 8):
                        d[i][m] = d[i][m] - u[i] * u[m]
                for i in range(j + 1, 8):
                    lines[i] = lines[i] - u[i] * lines[j]
                    other[i] = other[i] - u[i] * other[j]
            upper.append(packed(lines))
            inverse.append(packed(other))
            diag[1, base : base + 8, :] = inverse[s]
        for b in range(rank // size):

            @pl.when(block == b)
            def _():
                at, after = b * size, (b + 1) * size
                below = dot(a[after:, at:after], diag[1])
                a[after:, at:after] = below
                if after < rank:
                    a[after:, after:] = a[after:, after:] - dot(below, below[: rank - after])

    orth[...] = a[rank:]


def factor_call(gram, left):
    rank, rows = gram.shape[0], left.shape[0]
    vmem = pl.BlockSpec(memory_space=pltpu.VMEM)
    return pl.pallas_call(
        factor_kernel,
        out_shape=jax.ShapeDtypeStruct((rows, rank), jnp.float32),
        in_specs=[vmem] * 2,
        out_specs=vmem,
        scratch_shapes=[pltpu.VMEM((rank + rows, rank), jnp.float32), pltpu.VMEM((2, 128, 128), jnp.float32)],
        name="factor",
    )(gram, left)


def per_device(gradients, momentum, right_basis):
    mom, grad = momentum[0], gradients[0]
    rank = right_basis.shape[1]
    whole_rows = mom.shape[0] * lax.axis_size(Y) * lax.axis_size(K)
    gram_matrix, left_factor, merged_low = left_call(mom, grad, right_basis)
    orthonormal = factor_call(gram_matrix, left_factor)
    gathered, column_rms = right_call(merged_low, orthonormal)
    new_momentum, new_basis, update = final_call(
        gathered, column_rms, orthonormal, mom, grad, math.sqrt(whole_rows / rank)
    )
    return new_momentum[None], new_basis, update


def solution(mesh):
    torus = Mesh(
        mesh.devices.reshape(mesh.shape["grp"], mesh.shape["row"] // 2, 2, mesh.shape["col"]),
        (X, Y, K, Z),
    )
    return jax.shard_map(
        per_device,
        mesh=torus,
        in_specs=(P(X, ROW, Z), P(X, ROW, Z), P(Z, None)),
        out_specs=(P(X, ROW, Z), P(Z, None), P(ROW, Z)),
        check_vma=False,
    )
```

time: 168 us -> 156 us (0.929)
  Pallas kernels: 162 us -> 156 us
  local copies, waits for them, and re-layouts: 4.76 us -> 0 us
    unnamed x7 -> x0, local copies, waits for them, and re-layouts: 4.76 us -> none
    pallas_call x1 -> x2, Pallas kernels: 55 us -> 51.2 us  [the longest x1 46.4 us: right_call(): pl.pallas_call(functools.partial(right_kernel, nx, cols * nz), out_shape=...]
    pallas_call x1, Pallas kernels: 83.1 us -> 80.5 us  [left_call(): pl.pallas_call(left_kernel, out_shape=(jax.ShapeDtypeStruct((rank, rank),...]
where the time goes in v2:
time: 156 us
  Pallas kernels  156 us (100%)
    pallas_call x1, Pallas kernels, left_call(): pl.pallas_call(left_kernel, out_shape=(jax.ShapeDtypeStruct((rank, rank),...  80.5 us
    pallas_call x1, Pallas kernels, right_call(): pl.pallas_call(functools.partial(right_kernel, nx, cols * nz), out_shape=...  46.4 us
    pallas_call x1, Pallas kernels, factor_call(): pl.pallas_call(factor_kernel, out_shape=jax.ShapeDtypeStruct((rows, rank)...  23.7 us
    pallas_call x1, Pallas kernels, final_call(): pl.pallas_call(functools.partial(final_kernel, update_scale), grid=(cols...  4.83 us

profile of v2, /device:TPU:1, one launch (start us, length us, event | category | flops | bytes accessed | tf_op | source)
XLA Modules:
  0.0 156.2 jit_solution(5227598611940324203)
XLA Ops:
  0.6 80.5 %left.1 = (f32[512,512]{1,0:T(8,128)}, f32[192,512]{1,0:T(8,128)}, bf16[192,1536]{1,0:T(8,128)(2,1)}) custom-call(f32[192,1536]{1,0:T(8,128)} %bitcast.3, bf16[192,1536]{1,0:T(8,128)(2,1)} %bitcast.5, bf16[1536,512]{1,0:T(8,128)(2,1)} %basis.1), custom_call_target="tpu_custom_call" | custom-call | tf_op jit(solution)/shard_map/left/pallas_call | solution.py:176
  81.2 23.7 %factor.1.orth = f32[192,512]{1,0:T(8,128)} custom-call(f32[512,512]{1,0:T(8,128)} %get-tuple-element.12.gram, f32[192,512]{1,0:T(8,128)} %get-tuple-element.13.left), custom_call_target="tpu_custom_call" | custom-call | tf_op jit(solution)/shard_map/factor/pallas_call | solution.py:499
  104.9 46.4 %right.1 = (bf16[4,1536,128]{2,1,0:T(8,128)(2,1)}, f32[1,512]{1,0:T(1,128)}) custom-call(bf16[192,1536]{1,0:T(8,128)(2,1)} %get-tuple-element.11.low, f32[192,512]{1,0:T(8,128)} %factor.1.orth), custom_call_target="tpu_custom_call" | custom-call | tf_op jit(solution)/shard_map/right/pallas_call | solution.py:324
  151.3 4.8 %final.1 = (f32[192,1536]{1,0:T(8,128)}, bf16[1536,512]{1,0:T(8,128)(2,1)}, bf16[192,1536]{1,0:T(8,128)(2,1)}) custom-call(bf16[4,1536,128]{2,1,0:T(8,128)(2,1)} %get-tuple-element.14.nb, f32[1,512]{1,0:T(1,128)} %get-tuple-element.15.rms, f32[192,512]{1,0:T(8,128)} %factor.1.orth, f32[192,1536]{1,0:T(8,128)} %bitcast.4, bf16[192,1536]{1,0:T(8,128)(2,1)} %bitcast.6), custom_call_target="tpu_custom_call" | custom-call | tf_op jit(solution)/shard_map/final/pallas_call | solution.py:381

commit v3 on v2

--- a/solution.py
+++ b/solution.py
@@ -67,8 +67,8 @@
 
 
 def left_kernel(
-    mom, grad, basis, gram, left, low, part, xin, zpart, zin, lall, gall, gpair, kin, yall, gfull,
-    sx, sz, sza, sxa, sk, sy, sgz, sgx, sgk,
+    mom, grad, basis, gram, left, low, part, xin, zpart, zin, lall, gall, gpair, kin, gy, gyin, gfull,
+    sx, sz, sza, sxa, sk, sy, sgy, sgx, sgk,
 ):
     nx, ny, nz = lax.axis_size(X), lax.axis_size(Y), lax.axis_size(Z)
     g, y, k, c = (lax.axis_index(a) for a in (X, Y, K, Z))
@@ -122,25 +122,31 @@
             precision=lax.Precision.HIGHEST, preferred_element_type=jnp.float32,
         )
         gall[...] = outer if t == 0 else gall[...] + outer
-    strip = gall[pl.ds(pl.multiple_of(c * 8, 8), 8), :]
-    half = strip.shape[1] // 2
-    gpair[0] = strip[:, :half]
-    gpair[1] = strip[:, half:]
-    sent = started(scatter(gpair, kin, sk, K))
-    arrive(sent)
-    yall[y] = gpair[k] + kin[0]
-    sent = started(share(yall.at[y], sy, Y))
-    arrive(sent)
-    total = yall[0]
-    for j in range(1, ny):
-        total = total + yall[j]
-    parts = gfull.shape[1]
-    wide = half // parts
+    half = gall.shape[1] // 2
+    parts, wide = gpair.shape[0], gpair.shape[3]
+    deep = lanes // ny
     sent = []
     for u in range(parts):
-        gfull[k, u, g, c] = total[:, u * wide : (u + 1) * wide]
-        sent.append(started(share(gfull.at[k, u, g, c], sgz.at[u], Z)))
+        for h in range(2):
+            lane = h * half + u * wide
+            gpair[u, h] = gall[:, lane : lane + wide]
+        sent.append(started(scatter(gpair.at[u], kin.at[u], sk.at[u], K)))
     after = []
+    for u in range(parts):
+        arrive(sent[u])
+        total = gpair[u, k] + kin[u, 0]
+        for p in range(ny):
+            gy[u, p] = total[p * deep : (p + 1) * deep]
+        after.append(started(scatter(gy.at[u], gyin.at[u], sy.at[u], Y)))
+    sent, after = after, []
+    for u in range(parts):
+        arrive(sent[u])
+        own = gy[u, y]
+        for j in range(ny - 1):
+            own = own + gyin[u, j]
+        gfull[k, u, g, y] = own
+        after.append(started(share(gfull.at[k, u, g, y], sgy.at[u], Y)))
+    sent, after = after, []
     for u in range(parts):
         arrive(sent[u])
         after.append(started(share(gfull.at[k, u, g], sgx.at[u], X)))
@@ -150,13 +156,12 @@
         sent.append(started(share(gfull.at[k, u], sgk.at[u], K)))
     for u in range(parts):
         arrive(sent[u])
-    for h in range(2):
-        for u in range(parts):
+        for h in range(2):
             for b in range(nx):
-                for q in range(nz):
-                    at = (b * nz + q) * 8
+                for p in range(ny):
+                    at = b * lanes + p * deep
                     lane = h * half + u * wide
-                    gram[at : at + 8, lane : lane + wide] = gfull[h, u, b, q]
+                    gram[at : at + deep, lane : lane + wide] = gfull[h, u, b, p]
     depart(pending)
 
 
@@ -189,14 +194,15 @@
             pltpu.VMEM((chunks, nz - 1, 4, lanes), f32),
             pltpu.VMEM((chunks, nx, nz, 4, lanes), f32),
             pltpu.VMEM((lanes, rank), f32),
-            pltpu.VMEM((2, 8, half), f32),
-            pltpu.VMEM((1, 8, half), f32),
-            pltpu.VMEM((ny, 8, half), f32),
-            pltpu.VMEM((2, 2, nx, nz, 8, half // 2), f32),
+            pltpu.VMEM((2, 2, lanes, half // 2), f32),
+            pltpu.VMEM((2, 1, lanes, half // 2), f32),
+            pltpu.VMEM((2, ny, lanes // ny, half // 2), f32),
+            pltpu.VMEM((2, ny - 1, lanes // ny, half // 2), f32),
+            pltpu.VMEM((2, 2, nx, ny, lanes // ny, half // 2), f32),
             copies_of(chunks, nx), copies_of(chunks, nz), copies_of(chunks, nz), copies_of(chunks, nx),
-            copies_of(0, 2), copies_of(0, ny), copies_of(2, nz), copies_of(2, nx), copies_of(2, 2),
+            copies_of(2, 2), copies_of(2, ny), copies_of(2, ny), copies_of(2, nx), copies_of(2, 2),
         ],
-        compiler_params=pltpu.CompilerParams(collective_id=0, has_side_effects=True),
+        compiler_params=pltpu.CompilerParams(collective_id=0, has_side_effects=True, vmem_limit_bytes=24 << 20),
         name="left",
     )(mom, grad, basis)
 
@@ -348,7 +354,7 @@
             copies_of(chunks, nx), copies_of(chunks, 2),
             copies_of(0, nz), copies_of(0, 2), copies_of(0, nx), copies_of(0, ny),
         ],
-        compiler_params=pltpu.CompilerParams(collective_id=1, has_side_effects=True),
+        compiler_params=pltpu.CompilerParams(collective_id=1, has_side_effects=True, vmem_limit_bytes=24 << 20),
         name="right",
     )(low, orth)
 
@@ -395,6 +401,7 @@
         ],
         out_specs=(strip, pl.BlockSpec((step, rank), lambda i: (i, 0)), strip),
         scratch_shapes=[pltpu.VMEM((2 * rows, rank), bf16)],
+        compiler_params=pltpu.CompilerParams(vmem_limit_bytes=16 << 20),
         name="final",
     )(nb, rms, orth, mom, grad)
 
@@ -502,6 +509,7 @@
         in_specs=[vmem] * 2,
         out_specs=vmem,
         scratch_shapes=[pltpu.VMEM((rank + rows, rank), jnp.float32), pltpu.VMEM((2, 128, 128), jnp.float32)],
+        compiler_params=pltpu.CompilerParams(vmem_limit_bytes=16 << 20),
         name="factor",
     )(gram, left)
 

time: 156 us -> 145 us (0.929)
  Pallas kernels: 156 us -> 140 us
  local copies, waits for them, and re-layouts: 0 us -> 3.75 us
    pallas_call x1, Pallas kernels: 80.5 us -> 71.7 us  [left_call(): pl.pallas_call(left_kernel, out_shape=(jax.ShapeDtypeStruct((rank, rank),...]
    unnamed x0 -> x10, local copies, waits for them, and re-layouts: none -> 3.75 us
    pallas_call x1, Pallas kernels: 4.83 us -> 2.65 us  [final_call(): pl.pallas_call(functools.partial(final_kernel, update_scale), grid=(cols...]
    pallas_call x1, Pallas kernels: 46.4 us -> 44.2 us  [right_call(): pl.pallas_call(functools.partial(right_kernel, nx, cols * nz), out_shape=...]
    pallas_call x1, Pallas kernels: 23.7 us -> 21.7 us  [factor_call(): pl.pallas_call(factor_kernel, out_shape=jax.ShapeDtypeStruct((rows, rank)...]
where the time goes in v3:
time: 145 us
  Pallas kernels  140 us (97%)
  local copies, waits for them, and re-layouts  3.75 us (3%)
    pallas_call x1, Pallas kernels, left_call(): pl.pallas_call(left_kernel, out_shape=(jax.ShapeDtypeStruct((rank, rank),...  71.7 us
    pallas_call x1, Pallas kernels, right_call(): pl.pallas_call(functools.partial(right_kernel, nx, cols * nz), out_shape=...  44.2 us
    pallas_call x1, Pallas kernels, factor_call(): pl.pallas_call(factor_kernel, out_shape=jax.ShapeDtypeStruct((rows, rank)...  21.7 us
    unnamed x10, local copies, waits for them, and re-layouts  3.75 us

profile of v3, /device:TPU:1, one launch (start us, length us, event | category | flops | bytes accessed | tf_op | source)
XLA Modules:
  0.0 144.7 jit_solution(14609515039446149621)
XLA Ops:
  0.6 0.0 copy-start
  0.6 1.3 copy-done
  1.9 0.0 copy-start.2
  1.9 1.1 copy-done.2
  3.0 0.0 copy-start.4
  3.0 1.4 copy-done.4
  4.4 71.7 %left.1 = (f32[512,512]{1,0:T(8,128)S(1)}, f32[192,512]{1,0:T(8,128)S(1)}, bf16[192,1536]{1,0:T(8,128)(2,1)S(1)}) custom-call(f32[192,1536]{1,0:T(8,128)S(1)} %bitcast.3, bf16[192,1536]{1,0:T(8,128)(2,1)S(1)} %bitcast.5, bf16[1536,512]{1,0:T(8,128)(2,1)S(1)} %copy-done.4), custom_call_target="tpu_custom_call" | custom-call | tf_op jit(solution)/shard_map/left/pallas_call | solution.py:181
  76.0 0.0 copy-start.1
  76.1 0.0 copy-start.3
  76.1 21.7 %factor.1.orth = f32[192,512]{1,0:T(8,128)S(1)} custom-call(f32[512,512]{1,0:T(8,128)S(1)} %get-tuple-element.12.gram, f32[192,512]{1,0:T(8,128)S(1)} %get-tuple-element.13.left), custom_call_target="tpu_custom_call" | custom-call | tf_op jit(solution)/shard_map/factor/pallas_call | solution.py:506
  97.8 44.2 %right.1 = (bf16[4,1536,128]{2,1,0:T(8,128)(2,1)S(1)}, f32[1,512]{1,0:T(1,128)S(1)}) custom-call(bf16[192,1536]{1,0:T(8,128)(2,1)S(1)} %get-tuple-element.11.low, f32[192,512]{1,0:T(8,128)S(1)} %factor.1.orth), custom_call_target="tpu_custom_call" | custom-call | tf_op jit(solution)/shard_map/right/pallas_call | solution.py:330
  142.0 0.0 copy-done.1
  142.0 0.0 copy-done.3
  142.0 2.7 %final.1 = (f32[192,1536]{1,0:T(8,128)}, bf16[1536,512]{1,0:T(8,128)(2,1)}, bf16[192,1536]{1,0:T(8,128)(2,1)}) custom-call(bf16[4,1536,128]{2,1,0:T(8,128)(2,1)S(1)} %get-tuple-element.14.nb, f32[1,512]{1,0:T(1,128)S(1)} %get-tuple-element.15.rms, f32[192,512]{1,0:T(8,128)S(1)} %factor.1.orth, f32[192,1536]{1,0:T(8,128)S(1)} %bitcast.4, ...), custom_call_target="tpu_custom_call" | custom-call | tf_op jit(solution)/shard_map/final/pallas_call | solution.py:387
Async XLA Ops:
  0.6 1.3 copy-start
  1.9 1.1 copy-start.2
  3.0 1.4 copy-start.4
  76.0 66.0 %copy-start.1 = (f32[1,192,1536]{2,1,0:T(8,128)S(1)}, f32[1,192,1536]{2,1,0:T(8,128)}, u32[]{:S(2)}) copy-start(f32[1,192,1536]{2,1,0:T(8,128)} %param.4) | copy-start | bytes 3538948
  76.1 66.0 %copy-start.3 = (bf16[1,192,1536]{2,1,0:T(8,128)(2,1)S(1)}, bf16[1,192,1536]{2,1,0:T(8,128)(2,1)}, u32[]{:S(2)}) copy-start(bf16[1,192,1536]{2,1,0:T(8,128)(2,1)} %param.3) | copy-start | bytes 1769476

commit v4 on v3

--- a/solution.py
+++ b/solution.py
@@ -22,13 +22,16 @@
     return lax.rem(lax.axis_index(axis) + offset, lax.axis_size(axis))
 
 
-def meet(axes):
+def meet(axes, pairs=False):
     barrier = pltpu.get_barrier_semaphore()
     count = 0
     for axis in axes:
         for j in range(1, lax.axis_size(axis)):
             pl.semaphore_signal(barrier, inc=1, device_id={axis: peer_of(axis, j)}, device_id_type=MESH)
             count += 1
+    for j in range(1, lax.axis_size(X) if pairs else 1):
+        pl.semaphore_signal(barrier, inc=1, device_id={X: peer_of(X, j), K: peer_of(K, 1)}, device_id_type=MESH)
+        count += 1
     return lambda: pl.semaphore_wait(barrier, count)
 
 
@@ -54,6 +57,21 @@
         send(slot, slot, sems.at[0, j - 1], sems.at[1, j - 1], axis, peer_of(axis, j))
         for j in range(1, lax.axis_size(axis))
     ]
+
+
+def share_pair(slot, sems):
+    copies = []
+    for j in range(lax.axis_size(X)):
+        for i in range(2):
+            if i + j:
+                at = 2 * j + i - 1
+                copy = pltpu.make_async_remote_copy(
+                    src_ref=slot, dst_ref=slot, send_sem=sems.at[0, at], recv_sem=sems.at[1, at],
+                    device_id={X: peer_of(X, j), K: peer_of(K, i)}, device_id_type=MESH,
+                )
+                copy.start()
+                copies.append(copy)
+    return copies
 
 
 def arrive(copies):
@@ -77,18 +95,22 @@
     tall = 4 * nz
     merged_low = (mom[...] + grad[...].astype(jnp.float32)).astype(jnp.bfloat16)
     low[...] = merged_low
-    product = jnp.dot(merged_low, basis[...], preferred_element_type=jnp.float32)
-    for t in range(chunks):
-        for b in range(nx):
-            part[t, b] = product[t * tall : (t + 1) * tall, b * lanes : (b + 1) * lanes]
-    gathered()
     pending = []
 
     def started(copies):
         pending.extend(copies)
         return copies
 
-    sent = [started(scatter(part.at[t], xin.at[t], sx.at[t], X)) for t in range(chunks)]
+    sent = []
+    for t in range(chunks):
+        product = jnp.dot(
+            merged_low[t * tall : (t + 1) * tall], basis[...], preferred_element_type=jnp.float32
+        )
+        for b in range(nx):
+            part[t, b] = product[:, b * lanes : (b + 1) * lanes]
+        if t == 0:
+            gathered()
+        sent.append(started(scatter(part.at[t], xin.at[t], sx.at[t], X)))
     after = []
     for t in range(chunks):
         arrive(sent[t])
@@ -209,11 +231,11 @@
 
 def right_kernel(
     groups, whole_rows, low, orth, nb_out, rms_out, ksend, kin, mine, xsend, xin, ysum, ysend, yin, nb, low_left,
-    qz, qk, qx, qy, sk, sx, sy, say, sax, sak, sqz, sqk, sqx, sqy,
+    qz, qx, qy, sk, sx, sy, say, sax, sak, sqz, sqx, sqy,
 ):
     nx, ny, nz = lax.axis_size(X), lax.axis_size(Y), lax.axis_size(Z)
     g, y, k, c = (lax.axis_index(a) for a in (X, Y, K, Z))
-    gathered = meet((X, Y, K, Z))
+    gathered = meet((X, Y, K, Z), True)
     chunks, half, wide = ksend.shape
     f32, bf16 = jnp.float32, jnp.bfloat16
     low_left[...] = orth[...].astype(bf16)
@@ -235,16 +257,16 @@
         for t in range(chunks):
             ksend[t, pl.ds(pl.multiple_of(i * 128, 128), 128), :] = tile[:, t * wide : (t + 1) * wide]
 
-    gathered()
-    sent = [
-        started([send(ksend.at[t], kin.at[t], sk.at[t, 0, 0], sk.at[t, 1, 0], K, 1 - k)]) for t in range(chunks)
-    ]
-
     @pl.loop(0, half // 128)
     def _(i):
         tile = product(k * half + i * 128)
         for t in range(chunks):
             mine[t, pl.ds(pl.multiple_of(i * 128, 128), 128), :] = tile[:, t * wide : (t + 1) * wide]
+
+    gathered()
+    sent = [
+        started([send(ksend.at[t], kin.at[t], sk.at[t, 0, 0], sk.at[t, 1, 0], K, 1 - k)]) for t in range(chunks)
+    ]
 
     block = half // nx
     piece_rows = block // ny
@@ -297,13 +319,10 @@
         arrive(after[t])
         sent.append(started(share(nb.at[t, k], sak.at[t], K)))
     arrive(sent_q)
-    qx[g] = summed(qy, ny)
-    sent_q = started(share(qx.at[g], sqx, X))
+    qx[2 * g + k] = summed(qy, ny)
+    sent_q = started(share_pair(qx.at[2 * g + k], sqx))
     arrive(after[-1])
     sent.append(started(share(nb.at[chunks - 1, k], sak.at[chunks - 1], K)))
-    arrive(sent_q)
-    qk[k] = summed(qx, nx)
-    sent_q = started(share(qk.at[k], sqk, K))
     for t in range(chunks):
         arrive(sent[t])
         for h in range(2):
@@ -312,7 +331,7 @@
                     at = h * half + b * block + p * piece_rows
                     nb_out[t, at : at + piece_rows, :] = nb[t, h, b, p]
     arrive(sent_q)
-    rms_out[...] = jnp.sqrt(summed(qk, 2) / whole_rows + epsilon)
+    rms_out[...] = jnp.sqrt(summed(qx, 2 * nx) / whole_rows + epsilon)
     depart(pending)
 
 
@@ -347,12 +366,11 @@
             pltpu.VMEM((chunks, 2, nx, ny, piece, wide), bf16),
             pltpu.VMEM((rows, rank), bf16),
             pltpu.VMEM((nz, 1, rank), f32),
-            pltpu.VMEM((2, 1, rank), f32),
-            pltpu.VMEM((nx, 1, rank), f32),
+            pltpu.VMEM((2 * nx, 1, rank), f32),
             pltpu.VMEM((ny, 1, rank), f32),
             copies_of(chunks, 2), copies_of(chunks, nx), copies_of(chunks, ny), copies_of(chunks, ny),
             copies_of(chunks, nx), copies_of(chunks, 2),
-            copies_of(0, nz), copies_of(0, 2), copies_of(0, nx), copies_of(0, ny),
+            copies_of(0, nz), copies_of(0, 2 * nx), copies_of(0, ny),
         ],
         compiler_params=pltpu.CompilerParams(collective_id=1, has_side_effects=True, vmem_limit_bytes=24 << 20),
         name="right",

time: 145 us -> 144 us (level)
    pallas_call x1, Pallas kernels: 44.2 us -> 42.7 us  [right_call(): pl.pallas_call(functools.partial(right_kernel, nx, cols * nz), out_shape=...]
where the time goes in v4:
time: 144 us; the launch traced here: 143 us
  Pallas kernels  139 us (97%)
  local copies, waits for them, and re-layouts  3.75 us (3%)
    pallas_call x1, Pallas kernels, left_call(): pl.pallas_call(left_kernel, out_shape=(jax.ShapeDtypeStruct((rank, rank),...  71.8 us
    pallas_call x1, Pallas kernels, right_call(): pl.pallas_call(functools.partial(right_kernel, nx, cols * nz), out_shape=...  42.7 us
    pallas_call x1, Pallas kernels, factor_call(): pl.pallas_call(factor_kernel, out_shape=jax.ShapeDtypeStruct((rows, rank)...  21.7 us
    unnamed x10, local copies, waits for them, and re-layouts  3.75 us

profile of v4, /device:TPU:1, one launch (start us, length us, event | category | flops | bytes accessed | tf_op | source)
XLA Modules:
  0.0 143.3 jit_solution(11566473518186950703)
XLA Ops:
  0.6 0.0 copy-start
  0.6 1.3 copy-done
  1.9 0.0 copy-start.2
  1.9 1.1 copy-done.2
  3.0 0.0 copy-start.4
  3.0 1.4 copy-done.4
  4.4 71.8 %left.1 = (f32[512,512]{1,0:T(8,128)S(1)}, f32[192,512]{1,0:T(8,128)S(1)}, bf16[192,1536]{1,0:T(8,128)(2,1)S(1)}) custom-call(f32[192,1536]{1,0:T(8,128)S(1)} %bitcast.3, bf16[192,1536]{1,0:T(8,128)(2,1)S(1)} %bitcast.5, bf16[1536,512]{1,0:T(8,128)(2,1)S(1)} %copy-done.4), custom_call_target="tpu_custom_call" | custom-call | tf_op jit(solution)/shard_map/left/pallas_call | solution.py:203
  76.1 0.0 copy-start.1
  76.2 0.0 copy-start.3
  76.2 21.7 %factor.1.orth = f32[192,512]{1,0:T(8,128)S(1)} custom-call(f32[512,512]{1,0:T(8,128)S(1)} %get-tuple-element.12.gram, f32[192,512]{1,0:T(8,128)S(1)} %get-tuple-element.13.left), custom_call_target="tpu_custom_call" | custom-call | tf_op jit(solution)/shard_map/factor/pallas_call | solution.py:524
  97.9 42.7 %right.1 = (bf16[4,1536,128]{2,1,0:T(8,128)(2,1)S(1)}, f32[1,512]{1,0:T(1,128)S(1)}) custom-call(bf16[192,1536]{1,0:T(8,128)(2,1)S(1)} %get-tuple-element.11.low, f32[192,512]{1,0:T(8,128)S(1)} %factor.1.orth), custom_call_target="tpu_custom_call" | custom-call | tf_op jit(solution)/shard_map/right/pallas_call | solution.py:349
  140.6 0.0 copy-done.1
  140.6 0.0 copy-done.3
  140.6 2.6 %final.1 = (f32[192,1536]{1,0:T(8,128)}, bf16[1536,512]{1,0:T(8,128)(2,1)}, bf16[192,1536]{1,0:T(8,128)(2,1)}) custom-call(bf16[4,1536,128]{2,1,0:T(8,128)(2,1)S(1)} %get-tuple-element.14.nb, f32[1,512]{1,0:T(1,128)S(1)} %get-tuple-element.15.rms, f32[192,512]{1,0:T(8,128)S(1)} %factor.1.orth, f32[192,1536]{1,0:T(8,128)S(1)} %bitcast.4, ...), custom_call_target="tpu_custom_call" | custom-call | tf_op jit(solution)/shard_map/final/pallas_call | solution.py:405
Async XLA Ops:
  0.6 1.3 copy-start
  1.9 1.1 copy-start.2
  3.0 1.4 copy-start.4
  76.1 64.5 %copy-start.1 = (f32[1,192,1536]{2,1,0:T(8,128)S(1)}, f32[1,192,1536]{2,1,0:T(8,128)}, u32[]{:S(2)}) copy-start(f32[1,192,1536]{2,1,0:T(8,128)} %param.4) | copy-start | bytes 3538948
  76.2 64.5 %copy-start.3 = (bf16[1,192,1536]{2,1,0:T(8,128)(2,1)S(1)}, bf16[1,192,1536]{2,1,0:T(8,128)(2,1)}, u32[]{:S(2)}) copy-start(bf16[1,192,1536]{2,1,0:T(8,128)(2,1)} %param.3) | copy-start | bytes 1769476
